TPU v7x, 32 devices: a whole 2x2x4 slice. The times are simulated.
32 devices in a mesh: dp: 8 (over y, x, core), seq: 4 (over z).
Axes of the slice: x: 2, y: 2, z: 4, core: 2. Of those that a mesh axis runs over, the one named last changes fastest.
Arguments:
- grad_rows: bfloat16 [8, 320, 4, 1280], P('dp', 'seq'), may hold values from -6 to 6
- row_owner: int32 [8, 320, 1], P('dp', 'seq'), may hold values from 0 to 3; in each aligned block of 80 rows (0 to 79, 80 to 159, ..., all dimensions but the last counted through in order) at most 25 rows name the same one
- acts: bfloat16 [8, 4, 100, 4, 1280], P('dp', 'seq'), may hold values from -6 to 6
- xact: bfloat16 [8, 4, 100, 4, 1280], P('dp', 'seq'), may hold values from -72 to 72
- gamma: float32 [1280], replicated, may hold values from 0.25 to 1.75
- w_out: bfloat16 [1280, 1280], replicated, may hold values from -0.15625 to 0.15625
Outputs:
- attn_grad: bfloat16 [8, 4, 100, 4, 1280], P('dp', 'seq')
- weight_grad: float32 [1280, 1280], P('dp')
- gain_grad: float32 [1280], replicated
Inputs may be any that keep to these rules, and one draw needn't show every extreme that they name: `row_owner`: within the rows of one device (each aligned block of 80 rows) no owner is named more than 25 times, a bound that some block reaches.
All inputs are finite; a program needn't handle non-finite values.
Results may differ from a plain program's by a relative error of at most 0.0049.
Values may be sent and summed in bfloat16 or wider, within the bound.
A program may use at most 64 MiB of HBM per device.

v0:
```python
import jax
import jax.numpy as jnp
from jax import lax
from jax.sharding import PartitionSpec as P

epsilon = 1e-06


def slot_table(owners, buckets, capacity):
    picked = (owners[:, None] == jnp.arange(buckets, dtype=jnp.int32)[None, :]).astype(jnp.int32)
    before = jnp.cumsum(picked, axis=0) - picked
    ranking = jnp.sum(before * picked, axis=1)
    target = owners * capacity + ranking
    places = jnp.arange(buckets * capacity, dtype=jnp.int32)
    return (places[:, None] == target[None, :]).astype(jnp.bfloat16)


def norm_backward(upstream, inputs, gamma):
    values = inputs.astype(jnp.float32)
    inverse = lax.rsqrt(jnp.mean(values * values, axis=1, keepdims=True) + epsilon)
    normed = values * inverse
    gradient = upstream.astype(jnp.float32)
    gain_part = jnp.sum(gradient * normed, axis=0)
    scaled = gamma * gradient
    centre = jnp.mean(scaled * normed, axis=1, keepdims=True)
    patch_grad = (inverse * (scaled - normed * centre)).astype(jnp.bfloat16)
    return (patch_grad, gain_part)


def project_back(patch_grad, w_out):
    return lax.dot_general(
        patch_grad, w_out, (((1,), (1,)), ((), ())), preferred_element_type=jnp.float32
    ).astype(jnp.bfloat16)


def pick_rows(placing, stacked):
    return lax.dot_general(
        placing, stacked, (((0,), (0,)), ((), ())), preferred_element_type=jnp.float32
    ).astype(jnp.bfloat16)


def on_device(grad_rows, row_owner, acts, xact, gamma, w_out):
    seq_count = lax.axis_size("seq")
    slot_count = acts.shape[2]
    capacity = slot_count // seq_count
    patches = acts.shape[3]
    features = acts.shape[4]
    tok_rows = grad_rows.shape[1]
    placing = slot_table(row_owner[0, :, 0], seq_count, capacity)
    fetched = (
        lax.all_to_all(
            acts.reshape(seq_count, capacity, patches, features),
            "seq",
            split_axis=0,
            concat_axis=0,
            tiled=True,
        ),
        lax.all_to_all(
            xact.reshape(seq_count, capacity, patches, features),
            "seq",
            split_axis=0,
            concat_axis=0,
            tiled=True,
        ),
    )
    own_acts = pick_rows(placing, fetched[0].reshape(slot_count, patches * features))
    own_xact = pick_rows(placing, fetched[1].reshape(slot_count, patches * features))
    upstream = grad_rows.reshape(tok_rows * patches, features)
    act_rows = own_acts.reshape(tok_rows * patches, features)
    patch_grad, gain_part = norm_backward(
        upstream, own_xact.reshape(tok_rows * patches, features), gamma
    )
    attn_rows = project_back(patch_grad, w_out).reshape(tok_rows, patches * features)
    outgoing = jnp.dot(placing, attn_rows, preferred_element_type=jnp.float32).astype(jnp.bfloat16)
    returned = lax.all_to_all(
        outgoing.reshape(seq_count, capacity, patches, features),
        "seq",
        split_axis=0,
        concat_axis=0,
        tiled=True,
    )
    attn_grad = returned.reshape(acts.shape)
    weight_part = lax.psum_scatter(
        lax.dot_general(
            act_rows, patch_grad, (((0,), (0,)), ((), ())), preferred_element_type=jnp.float32
        ),
        "dp",
        scatter_dimension=0,
        tiled=True,
    )
    gain_sum = lax.psum(gain_part, ("dp", "seq"))
    weight_sum = lax.psum(weight_part, "seq")
    square_total = lax.psum(jnp.sum(weight_sum * weight_sum), "dp")
    norm_total = jnp.sqrt(square_total + jnp.sum(gain_sum * gain_sum) + epsilon)
    factor = jnp.float32(features) / norm_total
    return (attn_grad, weight_sum * factor, gain_sum * factor)


def solution(mesh):
    return jax.shard_map(
        on_device,
        mesh=mesh,
        in_specs=(
            P("dp", "seq", None, None),
            P("dp", "seq", None),
            P("dp", "seq", None, None, None),
            P("dp", "seq", None, None, None),
            P(),
            P(),
        ),
        out_specs=(P("dp", "seq", None, None, None), P("dp", None), P()),
        check_vma=False,
    )
```

profile of v0, /device:TPU:0, one launch (start us, length us, event | category | flops | bytes accessed | tf_op | source)
XLA Modules:
  0.0 224.4 jit_solution(17807708311614992503)
XLA Ops:
  7.2 6.6 %all-to-all-start = ((bf16[4,25,4,1280]{3,2,1,0:T(4,128)(2,1)}), bf16[4,25,4,1280]{3,2,1,0:T(4,128)(2,1)}, u32[]{:S(2)}, u32[]{:S(2)}) async-start(bf16[4,25,4,1280]{3,2,1,0:T(4,128)(2,1)} %bitcast.23), calls=%async_computation | async-start | bytes 2048000 | tf_op jit(solution)/shard_map/all_to_all | solution.py:58
  14.0 25.1 %all-to-all-done = bf16[4,25,4,1280]{3,2,1,0:T(4,128)(2,1)} async-done(((bf16[4,25,4,1280]{3,2,1,0:T(4,128)(2,1)}), bf16[4,25,4,1280]{3,2,1,0:T(4,128)(2,1)}, u32[]{:S(2)}, u32[]{:S(2)}) %all-to-all-start) | async-done | bytes 1024032 | tf_op jit(solution)/shard_map/all_to_all | solution.py:58
  39.1 4.2 %all-to-all-start.2 = ((bf16[4,25,4,1280]{3,2,1,0:T(4,128)(2,1)}), bf16[4,25,4,1280]{3,2,1,0:T(4,128)(2,1)}, u32[]{:S(2)}, u32[]{:S(2)}) async-start(bf16[4,25,4,1280]{3,2,1,0:T(4,128)(2,1)} %bitcast.24), calls=%async_computation.2 | async-start | bytes 2048000 | tf_op jit(solution)/shard_map/all_to_all | solution.py:51
  43.4 0.2 select_reduce_fusion
  43.6 1.6 pad
  45.4 1.6 fusion
  47.0 2.8 %reshape.145 = f32[320,1280]{1,0:T(8,128)} reshape(f32[80,5120]{1,0:T(8,128)} %fusion) | data formatting | bytes 3276800 | tf_op jit(solution)/shard_map/convert_element_type | solution.py:19
  49.8 3.0 %reshape.147 = f32[1,80,4,1280]{3,2,1,0:T(4,128)} reshape(f32[80,5120]{1,0:T(8,128)} %fusion) | data formatting | bytes 3276800 | tf_op jit(solution)/shard_map/convert_element_type | solution.py:19
  52.8 1.6 multiply_reduce_fusion.2
  54.6 2.7 %multiply_reduce_fusion = (f32[1280]{0:T(1024)S(1)}, f32[80,4]{1,0:T(8,128)S(1)}) fusion(f32[1,80,4,1280]{3,2,1,0:T(4,128)} %reshape.147, bf16[1,80,4,1280]{3,2,1,0:T(4,128)(2,1)} %param.6, f32[80,4]{1,0:T(8,128)S(1)} %rsqrt.14, f32[1280]{0:T(1024)S(1)} %copy-done.1), kind=kLoop, calls=%fused_computation.5 | loop fusion | flops 2865600 | bytes 2470400 | tf_op jit(solution)/shard_map/reduce_sum | solution.py:23
  57.3 10.9 %all-to-all-done.2 = bf16[4,25,4,1280]{3,2,1,0:T(4,128)(2,1)} async-done(((bf16[4,25,4,1280]{3,2,1,0:T(4,128)(2,1)}), bf16[4,25,4,1280]{3,2,1,0:T(4,128)(2,1)}, u32[]{:S(2)}, u32[]{:S(2)}) %all-to-all-start.2) | async-done | bytes 1024032 | tf_op jit(solution)/shard_map/all_to_all | solution.py:51
  68.2 1.6 pad.1
  69.9 1.3 convolution_convert_fusion.1
  71.3 2.3 %reshape.144 = bf16[320,1280]{1,0:T(8,128)(2,1)} reshape(bf16[80,5120]{1,0:T(8,128)(2,1)} %convolution_convert_fusion.1) | data formatting | bytes 1638400 | tf_op jit(solution)/shard_map/reshape | solution.py:69
  73.6 3.3 %multiply_convert_fusion = bf16[1,80,4,1280]{3,2,1,0:T(4,128)(2,1)} fusion(f32[1,80,4,1280]{3,2,1,0:T(4,128)} %reshape.147, bf16[1,80,4,1280]{3,2,1,0:T(4,128)(2,1)} %param.6, f32[80,4]{1,0:T(8,128)S(1)} %broadcast_multiply_fusion.1, f32[80,4]{1,0:T(8,128)S(1)} %rsqrt.14, f32[1280]{0:T(1024)S(1)} %copy-done.1), kind=kLoop, calls=%fused_computation.6 | loop fusion | flops 2867200 | bytes 3284480 | tf_op jit(solution)/shard_map/convert_element_type | solution.py:26
  76.9 2.3 %convert_element_type.72 = bf16[320,1280]{1,0:T(8,128)(2,1)} reshape(bf16[1,80,4,1280]{3,2,1,0:T(4,128)(2,1)} %multiply_convert_fusion) | data formatting | bytes 1638400 | tf_op jit(solution)/shard_map/convert_element_type | solution.py:26
  79.2 6.0 %fusion.8 = f32[1280,1280]{1,0:T(8,128)} fusion(bf16[320,1280]{1,0:T(8,128)(2,1)} %reshape.144, bf16[320,1280]{1,0:T(8,128)(2,1)} %convert_element_type.72), kind=kOutput, calls=%fused_computation.27 | convolution fusion | flops 1048576000 | bytes 8192000 | tf_op jit(solution)/shard_map/dot_general | solution.py:84
  85.3 2.6 %reshape.146 = f32[320,1280]{1,0:T(8,128)} reshape(bf16[1,80,4,1280]{3,2,1,0:T(4,128)(2,1)} %param.6) | data formatting | bytes 2457600 | tf_op jit(solution)/shard_map/convert_element_type | solution.py:22
  88.0 4.2 %convolution_convert_fusion.3 = bf16[320,1280]{1,0:T(8,128)(2,1)} fusion(bf16[1280,1280]{1,0:T(8,128)(2,1)S(1)} %copy-done, f32[320,1280]{1,0:T(8,128)} %reshape.145, f32[320,1280]{1,0:T(8,128)} %reshape.146, f32[320]{0:T(512)S(1)} %div.13, f32[1280]{0:T(1024)S(1)} %copy-done.1, f32[320]{0:T(512)S(1)} %add_rsqrt_fusion), kind=kOutput, calls=%fused_computation.4 | convolution fusion | flops 1051443200 | bytes 7380480 | tf_op jit(solution)/shard_map/dot_general | solution.py:31
  92.2 2.4 %reshape.139 = bf16[80,5120]{1,0:T(8,128)(2,1)} reshape(bf16[320,1280]{1,0:T(8,128)(2,1)} %convolution_convert_fusion.3) | data formatting | bytes 1638400 | tf_op jit(solution)/shard_map/reshape | solution.py:73
  94.5 2.7 %convolution_convert_fusion = bf16[100,5120]{1,0:T(8,128)(2,1)} fusion(bf16[80,5120]{1,0:T(8,128)(2,1)} %reshape.139, s32[80]{0:T(128)S(1)} %multiply_add_fusion), kind=kOutput, calls=%fused_computation | convolution fusion | flops 82440000 | bytes 1843520 | tf_op jit(solution)/shard_map/dot_general | solution.py:74
  97.2 3.2 %reshape.140 = bf16[4,25,4,1280]{3,2,1,0:T(4,128)(2,1)} reshape(bf16[100,5120]{1,0:T(8,128)(2,1)} %convolution_convert_fusion) | data formatting | bytes 2048000 | tf_op jit(solution)/shard_map/reshape | solution.py:76
  100.4 4.2 %all-to-all-start.1 = ((bf16[4,25,4,1280]{3,2,1,0:T(4,128)(2,1)}), bf16[4,25,4,1280]{3,2,1,0:T(4,128)(2,1)}, u32[]{:S(2)}, u32[]{:S(2)}) async-start(bf16[4,25,4,1280]{3,2,1,0:T(4,128)(2,1)} %reshape.140), calls=%async_computation.1 | async-start | bytes 2048000 | tf_op jit(solution)/shard_map/all_to_all | solution.py:75
  104.7 42.8 %reduce-scatter.2.cloned.1.call-done = f32[160,1280]{1,0:T(8,128)} async-done(((f32[1280,1280]{1,0:T(8,128)}), f32[160,1280]{1,0:T(8,128)}) %reduce-scatter.2.cloned.1.call-update) | async-done | bytes 819216 | tf_op jit(solution)/shard_map/reduce_scatter | solution.py:83
  147.6 40.5 %psum.23 = f32[1280]{0:T(1024)S(1)} all-reduce(f32[1280]{0:T(1024)S(1)} %get-tuple-element.3), channel_id=1, replica_groups=mesh['dp'=8,'seq'=4] {'dp','seq'}, use_global_device_ids=true, to_apply=%region_9.10 | all-reduce | flops 1280 | bytes 10240 | tf_op jit(solution)/shard_map/psum | solution.py:91
  188.1 0.6 multiply_reduce_fusion.4
  188.7 6.7 %all-reduce.2.cloned.1.call-done = f32[160,1280]{1,0:T(8,128)} async-done(((f32[160,1280]{1,0:T(8,128)}), f32[160,1280]{1,0:T(8,128)}) %all-reduce.2.cloned.1.call-update) | async-done | bytes 819216 | tf_op jit(solution)/shard_map/psum | solution.py:92
  195.4 2.0 multiply_reduce_fusion.3
  197.3 13.7 %psum.22 = f32[]{:T(128)} all-reduce(f32[]{:T(128)} %multiply_reduce_fusion.3), channel_id=1, replica_groups=mesh['dp'=8,'seq'=4] {'dp'}, use_global_device_ids=true, to_apply=%region_7.8 | all-reduce | flops 1 | bytes 8 | tf_op jit(solution)/shard_map/psum | solution.py:93
  212.4 0.6 broadcast_multiply_fusion.2
  213.0 2.1 broadcast_multiply_fusion
  215.1 2.5 %copy.13 = bf16[1,1,100,4,1280]{4,3,2,1,0:T(4,128)(2,1)} copy(bf16[1,1,100,4,1280]{4,3,2,1,0:T(4,128)(2,1)} %bitcast.2) | data formatting | bytes 2048000
  (20 shorter events, 0.8 us)
Async XLA Ops:
  7.2 80.8 %copy-start = (bf16[1280,1280]{1,0:T(8,128)(2,1)S(1)}, bf16[1280,1280]{1,0:T(8,128)(2,1)}, u32[]{:S(2)}) copy-start(bf16[1280,1280]{1,0:T(8,128)(2,1)} %param.11) | copy-start | bytes 9830404
  7.2 6.6 %copy-start.2 = (s32[1,80,1]{1,2,0:T(1,128)S(1)}, s32[1,80,1]{1,2,0:T(1,128)}, u32[]{:S(2)}) copy-start(s32[1,80,1]{1,2,0:T(1,128)} %param.7) | copy-start | bytes 964
  7.2 31.9 %all-to-all-start = ((bf16[4,25,4,1280]{3,2,1,0:T(4,128)(2,1)}), bf16[4,25,4,1280]{3,2,1,0:T(4,128)(2,1)}, u32[]{:S(2)}, u32[]{:S(2)}) async-start(bf16[4,25,4,1280]{3,2,1,0:T(4,128)(2,1)} %bitcast.23), calls=%async_computation | async-start | bytes 2048000 | tf_op jit(solution)/shard_map/all_to_all | solution.py:58
  39.1 29.1 %all-to-all-start.2 = ((bf16[4,25,4,1280]{3,2,1,0:T(4,128)(2,1)}), bf16[4,25,4,1280]{3,2,1,0:T(4,128)(2,1)}, u32[]{:S(2)}, u32[]{:S(2)}) async-start(bf16[4,25,4,1280]{3,2,1,0:T(4,128)(2,1)} %bitcast.24), calls=%async_computation.2 | async-start | bytes 2048000 | tf_op jit(solution)/shard_map/all_to_all | solution.py:51
  43.4 104.2 %reduce-scatter.2.cloned.1.call-start = ((), (), s32[]{:S(2)}) async-start(), calls=%async_computation.4 | async-start | bytes 7372800 | tf_op jit(solution)/shard_map/reduce_scatter | solution.py:83
  52.8 1.8 copy-start.1
  100.4 96.9 %all-to-all-start.1 = ((bf16[4,25,4,1280]{3,2,1,0:T(4,128)(2,1)}), bf16[4,25,4,1280]{3,2,1,0:T(4,128)(2,1)}, u32[]{:S(2)}, u32[]{:S(2)}) async-start(bf16[4,25,4,1280]{3,2,1,0:T(4,128)(2,1)} %reshape.140), calls=%async_computation.1 | async-start | bytes 2048000 | tf_op jit(solution)/shard_map/all_to_all | solution.py:75
  104.7 90.7 %all-reduce.2.cloned.1.call-start = ((), (), s32[]{:S(2)}) async-start(), calls=%async_computation.5 | async-start | bytes 1638400 | tf_op jit(solution)/shard_map/psum | solution.py:92
Sparse Core Ops, SparseCore 0:
  85.4 62.0 reduce-scatter.1
  149.9 45.4 all-reduce.1
where the time goes:
time: 225 us; the launch traced here: 224 us
  waiting for transfers between devices  85.5 us (38%)
  blocking collectives  54.2 us (24%)
  local copies, waits for them, and re-layouts  24.8 us (11%)
  matrix products  15.9 us (7%)
  between operations  15.5 us (7%)
  starting transfers between devices  15.2 us (7%)
  other arithmetic  13.3 us (6%)
    reduce_scatter x1, waiting for transfers between devices, on_device(): lax.psum_scatter(lax.dot_general(act_rows, patch_grad, (((0,), (0,)), (()...  42.8 us
    psum x1, blocking collectives, on_device(): gain_sum = lax.psum(gain_part, ('dp', 'seq'))  40.5 us
    all_to_all x1, waiting for transfers between devices, on_device(): lax.all_to_all(xact.reshape(seq_count, capacity, patches, features), 'seq...  25.1 us
    psum x1, blocking collectives, on_device(): square_total = lax.psum(jnp.sum(weight_sum * weight_sum), 'dp')  13.7 us
    all_to_all x1, waiting for transfers between devices, on_device(): lax.all_to_all(acts.reshape(seq_count, capacity, patches, features), 'seq...  10.9 us
    psum x1, waiting for transfers between devices, on_device(): weight_sum = lax.psum(weight_part, 'seq')  6.7 us
    all_to_all x1, starting transfers between devices, on_device(): lax.all_to_all(xact.reshape(seq_count, capacity, patches, features), 'seq...  6.62 us
    unnamed x11, local copies, waits for them, and re-layouts  6.05 us
  transfers between devices with their start and end apart: 5, of which 4 were waited for; matrix products, arithmetic and copies ran while one was open for 14% of the time, Pallas kernels for 0%

commit v1 on v0

--- a/solution.py
+++ b/solution.py
@@ -88,7 +88,7 @@
         scatter_dimension=0,
         tiled=True,
     )
-    gain_sum = lax.psum(gain_part, ("dp", "seq"))
+    gain_sum = jnp.sum(lax.all_gather(gain_part, ("dp", "seq")), axis=0)
     weight_sum = lax.psum(weight_part, "seq")
     square_total = lax.psum(jnp.sum(weight_sum * weight_sum), "dp")
     norm_total = jnp.sqrt(square_total + jnp.sum(gain_sum * gain_sum) + epsilon)

time: 225 us -> 246 us (1.093)
  blocking collectives: 54.2 us -> 81.5 us
  waiting for transfers between devices: 85.5 us -> 78.8 us
    all_gather x0 -> x1, blocking collectives: none -> 69.1 us  [on_device(): gain_sum = jnp.sum(lax.all_gather(gain_part, ('dp', 'seq')), axis=0)]
    psum x1 -> x0, blocking collectives: 40.5 us -> none  [on_device(): gain_sum = lax.psum(gain_part, ('dp', 'seq'))]
    psum x1, waiting for transfers between devices: 6.7 us -> 0.01 us  [on_device(): weight_sum = lax.psum(weight_part, 'seq')]
    unnamed x11 -> x12, local copies, waits for them, and re-layouts: 6.05 us -> 6.05 us
  transfers between devices with their start and end apart: 5 -> 5, of which waited for: 4 -> 3; matrix products, arithmetic and copies ran while one was open for 14% -> 13% of each run, Pallas kernels for 0% -> 0%
where the time goes in v1:
time: 246 us; the launch traced here: 245 us
  blocking collectives  81.5 us (33%)
  waiting for transfers between devices  78.8 us (32%)
  local copies, waits for them, and re-layouts  24.8 us (10%)
  matrix products  15.9 us (6%)
  between operations  15.5 us (6%)
  starting transfers between devices  15.2 us (6%)
  other arithmetic  13.5 us (5%)
    all_gather x1, blocking collectives, on_device(): gain_sum = jnp.sum(lax.all_gather(gain_part, ('dp', 'seq')), axis=0)  69.1 us
    reduce_scatter x1, waiting for transfers between devices, on_device(): lax.psum_scatter(lax.dot_general(act_rows, patch_grad, (((0,), (0,)), (()...  42.8 us
    all_to_all x1, waiting for transfers between devices, on_device(): lax.all_to_all(xact.reshape(seq_count, capacity, patches, features), 'seq...  25.1 us
    psum x1, blocking collectives, on_device(): square_total = lax.psum(jnp.sum(weight_sum * weight_sum), 'dp')  12.4 us
    all_to_all x1, waiting for transfers between devices, on_device(): lax.all_to_all(acts.reshape(seq_count, capacity, patches, features), 'seq...  10.9 us
    all_to_all x1, starting transfers between devices, on_device(): lax.all_to_all(xact.reshape(seq_count, capacity, patches, features), 'seq...  6.62 us
    unnamed x12, local copies, waits for them, and re-layouts  6.05 us
    dot_general x1, matrix products, on_device(): lax.dot_general(act_rows, patch_grad, (((0,), (0,)), ((), ())), preferred...  6.03 us
  transfers between devices with their start and end apart: 5, of which 3 were waited for; matrix products, arithmetic and copies ran while one was open for 13% of the time, Pallas kernels for 0%

profile of v1, /device:TPU:0, one launch (start us, length us, event | category | flops | bytes accessed | tf_op | source)
XLA Modules:
  0.0 245.1 jit_solution(11323477373315361755)
XLA Ops:
  7.2 6.6 %all-to-all-start = ((bf16[4,25,4,1280]{3,2,1,0:T(4,128)(2,1)}), bf16[4,25,4,1280]{3,2,1,0:T(4,128)(2,1)}, u32[]{:S(2)}, u32[]{:S(2)}) async-start(bf16[4,25,4,1280]{3,2,1,0:T(4,128)(2,1)} %bitcast.23), calls=%async_computation | async-start | bytes 2048000 | tf_op jit(solution)/shard_map/all_to_all | solution.py:58
  14.0 25.1 %all-to-all-done = bf16[4,25,4,1280]{3,2,1,0:T(4,128)(2,1)} async-done(((bf16[4,25,4,1280]{3,2,1,0:T(4,128)(2,1)}), bf16[4,25,4,1280]{3,2,1,0:T(4,128)(2,1)}, u32[]{:S(2)}, u32[]{:S(2)}) %all-to-all-start) | async-done | bytes 1024032 | tf_op jit(solution)/shard_map/all_to_all | solution.py:58
  39.1 4.2 %all-to-all-start.2 = ((bf16[4,25,4,1280]{3,2,1,0:T(4,128)(2,1)}), bf16[4,25,4,1280]{3,2,1,0:T(4,128)(2,1)}, u32[]{:S(2)}, u32[]{:S(2)}) async-start(bf16[4,25,4,1280]{3,2,1,0:T(4,128)(2,1)} %bitcast.24), calls=%async_computation.2 | async-start | bytes 2048000 | tf_op jit(solution)/shard_map/all_to_all | solution.py:51
  43.4 0.2 select_reduce_fusion
  43.6 1.6 pad
  45.2 0.1 copy.9
  45.4 1.6 fusion
  47.0 2.8 %reshape.145 = f32[320,1280]{1,0:T(8,128)} reshape(f32[80,5120]{1,0:T(8,128)} %fusion) | data formatting | bytes 3276800 | tf_op jit(solution)/shard_map/convert_element_type | solution.py:19
  49.8 3.0 %reshape.147 = f32[1,80,4,1280]{3,2,1,0:T(4,128)} reshape(f32[80,5120]{1,0:T(8,128)} %fusion) | data formatting | bytes 3276800 | tf_op jit(solution)/shard_map/convert_element_type | solution.py:19
  52.8 1.6 multiply_reduce_fusion.2
  54.6 2.7 %multiply_reduce_fusion = (f32[1280]{0:T(1024)S(1)}, f32[80,4]{1,0:T(8,128)S(1)}) fusion(f32[1,80,4,1280]{3,2,1,0:T(4,128)} %reshape.147, bf16[1,80,4,1280]{3,2,1,0:T(4,128)(2,1)} %param.6, f32[80,4]{1,0:T(8,128)S(1)} %rsqrt.14, f32[1280]{0:T(1024)S(1)} %copy-done.1), kind=kLoop, calls=%fused_computation.5 | loop fusion | flops 2865600 | bytes 2470400 | tf_op jit(solution)/shard_map/reduce_sum | solution.py:23
  57.3 10.9 %all-to-all-done.2 = bf16[4,25,4,1280]{3,2,1,0:T(4,128)(2,1)} async-done(((bf16[4,25,4,1280]{3,2,1,0:T(4,128)(2,1)}), bf16[4,25,4,1280]{3,2,1,0:T(4,128)(2,1)}, u32[]{:S(2)}, u32[]{:S(2)}) %all-to-all-start.2) | async-done | bytes 1024032 | tf_op jit(solution)/shard_map/all_to_all | solution.py:51
  68.2 1.6 pad.1
  69.9 1.3 convolution_convert_fusion.1
  71.3 2.3 reshape.144
  73.6 3.3 %multiply_convert_fusion = bf16[1,80,4,1280]{3,2,1,0:T(4,128)(2,1)} fusion(f32[1,80,4,1280]{3,2,1,0:T(4,128)} %reshape.147, bf16[1,80,4,1280]{3,2,1,0:T(4,128)(2,1)} %param.6, f32[80,4]{1,0:T(8,128)S(1)} %broadcast_multiply_fusion.1, f32[80,4]{1,0:T(8,128)S(1)} %rsqrt.14, f32[1280]{0:T(1024)S(1)} %copy-done.1), kind=kLoop, calls=%fused_computation.6 | loop fusion | flops 2867200 | bytes 3284480 | tf_op jit(solution)/shard_map/convert_element_type | solution.py:26
  76.9 2.3 convert_element_type.72
  79.2 6.0 %fusion.8 = f32[1280,1280]{1,0:T(8,128)} fusion(bf16[320,1280]{1,0:T(8,128)(2,1)} %reshape.144, bf16[320,1280]{1,0:T(8,128)(2,1)} %convert_element_type.72), kind=kOutput, calls=%fused_computation.27 | convolution fusion | flops 1048576000 | bytes 8192000 | tf_op jit(solution)/shard_map/dot_general | solution.py:84
  85.3 2.6 %reshape.146 = f32[320,1280]{1,0:T(8,128)} reshape(bf16[1,80,4,1280]{3,2,1,0:T(4,128)(2,1)} %param.6) | data formatting | bytes 2457600 | tf_op jit(solution)/shard_map/convert_element_type | solution.py:22
  88.0 4.2 %convolution_convert_fusion.3 = bf16[320,1280]{1,0:T(8,128)(2,1)} fusion(bf16[1280,1280]{1,0:T(8,128)(2,1)S(1)} %copy-done, f32[320,1280]{1,0:T(8,128)} %reshape.145, f32[320,1280]{1,0:T(8,128)} %reshape.146, f32[320]{0:T(512)S(1)} %div.13, f32[1280]{0:T(1024)S(1)} %copy-done.1, f32[320]{0:T(512)S(1)} %add_rsqrt_fusion), kind=kOutput, calls=%fused_computation.4 | convolution fusion | flops 1051443200 | bytes 7380480 | tf_op jit(solution)/shard_map/dot_general | solution.py:31
  92.2 2.4 reshape.139
  94.5 2.7 %convolution_convert_fusion = bf16[100,5120]{1,0:T(8,128)(2,1)} fusion(bf16[80,5120]{1,0:T(8,128)(2,1)} %reshape.139, s32[80]{0:T(128)S(1)} %multiply_add_fusion), kind=kOutput, calls=%fused_computation | convolution fusion | flops 82440000 | bytes 1843520 | tf_op jit(solution)/shard_map/dot_general | solution.py:74
  97.2 3.2 %reshape.140 = bf16[4,25,4,1280]{3,2,1,0:T(4,128)(2,1)} reshape(bf16[100,5120]{1,0:T(8,128)(2,1)} %convolution_convert_fusion) | data formatting | bytes 2048000 | tf_op jit(solution)/shard_map/reshape | solution.py:76
  100.4 4.2 %all-to-all-start.1 = ((bf16[4,25,4,1280]{3,2,1,0:T(4,128)(2,1)}), bf16[4,25,4,1280]{3,2,1,0:T(4,128)(2,1)}, u32[]{:S(2)}, u32[]{:S(2)}) async-start(bf16[4,25,4,1280]{3,2,1,0:T(4,128)(2,1)} %reshape.140), calls=%async_computation.1 | async-start | bytes 2048000 | tf_op jit(solution)/shard_map/all_to_all | solution.py:75
  104.7 42.8 %reduce-scatter.2.cloned.1.call-done = f32[160,1280]{1,0:T(8,128)} async-done(((f32[1280,1280]{1,0:T(8,128)}), f32[160,1280]{1,0:T(8,128)}) %reduce-scatter.2.cloned.1.call-update) | async-done | bytes 819216 | tf_op jit(solution)/shard_map/reduce_scatter | solution.py:83
  147.6 69.1 %all-gather.1 = f32[32,1,1280]{2,1,0:T(1,128)S(1)} all-gather(f32[1,1,1280]{2,1,0:T(1,128)S(1)} %reshape.149), channel_id=2, replica_groups=mesh['dp'=8,'seq'=4] {'dp','seq'}, dimensions={0}, use_global_device_ids=true | all-gather | bytes 168960 | tf_op jit(solution)/shard_map/all_gather | solution.py:91
  216.8 0.6 multiply_reduce_fusion.4
  217.4 2.0 multiply_reduce_fusion.3
  219.3 12.4 %psum.15 = f32[]{:T(128)} all-reduce(f32[]{:T(128)} %multiply_reduce_fusion.3), channel_id=1, replica_groups=mesh['dp'=8,'seq'=4] {'dp'}, use_global_device_ids=true, to_apply=%region_7.8 | all-reduce | flops 1 | bytes 8 | tf_op jit(solution)/shard_map/psum | solution.py:93
  233.1 0.6 broadcast_multiply_fusion.2
  233.7 2.1 broadcast_multiply_fusion
  235.8 2.5 %copy.13 = bf16[1,1,100,4,1280]{4,3,2,1,0:T(4,128)(2,1)} copy(bf16[1,1,100,4,1280]{4,3,2,1,0:T(4,128)(2,1)} %bitcast.2) | data formatting | bytes 2048000
  (22 shorter events, 0.8 us)
Async XLA Ops:
  7.2 80.8 %copy-start = (bf16[1280,1280]{1,0:T(8,128)(2,1)S(1)}, bf16[1280,1280]{1,0:T(8,128)(2,1)}, u32[]{:S(2)}) copy-start(bf16[1280,1280]{1,0:T(8,128)(2,1)} %param.11) | copy-start | bytes 9830404
  7.2 6.6 %copy-start.2 = (s32[1,80,1]{1,2,0:T(1,128)S(1)}, s32[1,80,1]{1,2,0:T(1,128)}, u32[]{:S(2)}) copy-start(s32[1,80,1]{1,2,0:T(1,128)} %param.7) | copy-start | bytes 964
  7.2 31.9 %all-to-all-start = ((bf16[4,25,4,1280]{3,2,1,0:T(4,128)(2,1)}), bf16[4,25,4,1280]{3,2,1,0:T(4,128)(2,1)}, u32[]{:S(2)}, u32[]{:S(2)}) async-start(bf16[4,25,4,1280]{3,2,1,0:T(4,128)(2,1)} %bitcast.23), calls=%async_computation | async-start | bytes 2048000 | tf_op jit(solution)/shard_map/all_to_all | solution.py:58
  39.1 29.1 %all-to-all-start.2 = ((bf16[4,25,4,1280]{3,2,1,0:T(4,128)(2,1)}), bf16[4,25,4,1280]{3,2,1,0:T(4,128)(2,1)}, u32[]{:S(2)}, u32[]{:S(2)}) async-start(bf16[4,25,4,1280]{3,2,1,0:T(4,128)(2,1)} %bitcast.24), calls=%async_computation.2 | async-start | bytes 2048000 | tf_op jit(solution)/shard_map/all_to_all | solution.py:51
  43.4 104.2 %reduce-scatter.2.cloned.1.call-start = ((), (), s32[]{:S(2)}) async-start(), calls=%async_computation.4 | async-start | bytes 7372800 | tf_op jit(solution)/shard_map/reduce_scatter | solution.py:83
  52.8 1.8 copy-start.1
  100.4 118.9 %all-to-all-start.1 = ((bf16[4,25,4,1280]{3,2,1,0:T(4,128)(2,1)}), bf16[4,25,4,1280]{3,2,1,0:T(4,128)(2,1)}, u32[]{:S(2)}, u32[]{:S(2)}) async-start(bf16[4,25,4,1280]{3,2,1,0:T(4,128)(2,1)} %reshape.140), calls=%async_computation.1 | async-start | bytes 2048000 | tf_op jit(solution)/shard_map/all_to_all | solution.py:75
  104.7 112.7 %all-reduce.2.cloned.1.call-start = ((), (), s32[]{:S(2)}) async-start(), calls=%async_computation.5 | async-start | bytes 1638400 | tf_op jit(solution)/shard_map/psum | solution.py:92
Sparse Core Ops, SparseCore 0:
  85.4 62.0 reduce-scatter.1
  149.9 46.1 all-reduce.1
